TPU v7x, 256 devices: a 4x2x16 block of a 4x16x16 slice. The times are simulated.
256 devices in a mesh: ens: 2 (over y), gx: 128 (over x, z, core).
Axes of the slice: x: 4, y: 2, z: 16, core: 2. Of those that a mesh axis runs over, the one named last changes fastest.
The devices are a block of a 4x16x16 slice.
Arguments:
- model_state: float32 [8, 4, 2560, 2560], P('ens', None, 'gx'), parts along dimension 0, may hold values from -6 to 6
- driving: float32 [8, 4, 2560, 2560], P('ens', None, 'gx'), parts along dimension 0, may hold values from -12 to 12
- mode_east: int32 [30], replicated, may hold values from 1 to 60, as said below
- mode_north: int32 [30], replicated, may hold values from 1 to 60, as said below
- level_class: int32 [4], replicated, may hold values from 0 to 7
- nudge_table: float32 [8, 4], replicated, may hold values from 0.05 to 0.5
Outputs:
- nudged: float32 [8, 4, 2560, 2560], P('ens', None, 'gx'), parts along dimension 0
- residual_log: float32 [8, 4], P('ens'), parts along dimension 0
There are 2 independent parts, one for each index of `ens`. A program takes and returns all parts, laid end to end along the dimension named above; an argument that names none is the same for every part. Nothing has to cross between parts.
Inputs may be any that keep to these rules, and one draw needn't show every extreme that they name: `mode_east`: 30 distinct wavenumbers in increasing order, the first 1 and the last 60. `mode_north`: 30 distinct wavenumbers in increasing order, the first 1 and the last 60.
All inputs are finite; a program needn't handle non-finite values.
Results may differ from a plain program's by a relative error of at most 0.0001.
Values sent between devices are 32-bit elements; how exact they have to be, the bound alone decides.
A program may use at most 128 MiB of HBM per device.

v0:
```python
import jax
import jax.numpy as jnp
from jax import lax
from jax.sharding import Mesh
from jax.sharding import PartitionSpec as P

ITERS = 4
GX = ("gx_0", "gx_1", "gx_2")
DIFFUSION = 0.24


def by_axis(value, axes):
    for axis in axes:
        value = lax.psum(value, axis)
    return value


def extended_2(cells, sides, width):
    for axis, dim in sides:
        count = lax.axis_size(axis)
        ends = count - 1
        head = lax.slice_in_dim(cells, 0, width, axis=dim)
        tail = lax.slice_in_dim(cells, cells.shape[dim] - width, cells.shape[dim], axis=dim)
        cells = jnp.concatenate(
            [
                lax.ppermute(tail, axis, [(i, (i + 1) % count) for i in range(ends)]),
                cells,
                lax.ppermute(head, axis, [((i + 1) % count, i) for i in range(ends)]),
            ],
            axis=dim,
        )
    return cells


def sine_table(wavenums, first_cell, span_cols, grid_cells):
    places = first_cell + lax.iota(jnp.int32, span_cols) + 1
    phases = wavenums[:, None] * places[None, :] % (2 * (grid_cells + 1))
    return jnp.sin(phases.astype(jnp.float32) * (jnp.pi / (grid_cells + 1)))


def laplace(extended):
    centre = extended[:, :, 1:-1]
    padded = jnp.pad(centre, ((0, 0), (0, 0), (0, 0), (1, 1)))
    return (
        extended[:, :, 2:]
        + extended[:, :, :-2]
        + padded[:, :, :, 2:]
        + padded[:, :, :, :-2]
        - 4.0 * centre
    )


def local(model_state, driving, mode_east, mode_north, level_class, nudge_table):
    fields, levels, columns, north_cells = model_state.shape
    tiles = lax.axis_size(GX)
    first_col = lax.axis_index(GX) * columns
    total_east = columns * tiles
    scale_norm = 4.0 / ((total_east + 1) * (north_cells + 1))
    cell_count = float(levels * total_east * north_cells)
    table_north = sine_table(mode_north, 0, north_cells, north_cells)
    table_own = sine_table(mode_east, first_col, columns, total_east)
    one_hot = (level_class[:, None] == lax.iota(jnp.int32, nudge_table.shape[0])[None, :]).astype(
        jnp.float32
    )
    weights = jnp.dot(one_hot, nudge_table, precision=lax.Precision.HIGHEST).T[:, :, None, None]
    records = []
    extended = extended_2(model_state, ((GX, 2),), ITERS)
    for substep in range(ITERS):
        reach_now = ITERS - substep
        current = extended[:, :, reach_now : reach_now + columns]
        along_north = jnp.dot(
            (driving - current).reshape(-1, north_cells),
            table_north.T,
            precision=lax.Precision.HIGHEST,
        )
        along_north = along_north.reshape(fields, levels, columns, -1)
        mode_partial_value = (
            jnp.einsum("flxb,ax->flab", along_north, table_own, precision=lax.Precision.HIGHEST)
            * scale_norm
        )
        coeffs = by_axis(mode_partial_value, GX)
        lead_col = first_col - (reach_now - 1)
        span_cols = columns + 2 * (reach_now - 1)
        table_wide = sine_table(mode_east, lead_col, span_cols, total_east)
        global_col = lead_col + lax.iota(jnp.int32, span_cols)
        inside = ((global_col >= 0) & (global_col < total_east))[None, None, :, None]
        partial_value = jnp.einsum(
            "flab,ax->flxb", coeffs, table_wide, precision=lax.Precision.HIGHEST
        )
        rebuild_span_cols = table_wide.shape[1]
        flat = jnp.dot(
            partial_value.reshape(-1, partial_value.shape[-1]),
            table_north,
            precision=lax.Precision.HIGHEST,
        )
        updated = (
            extended[:, :, 1:-1]
            + flat.reshape(fields, levels, rebuild_span_cols, north_cells) * weights
            + DIFFUSION * laplace(extended)
        )
        extended = jnp.where(inside, updated, 0.0)
        current = extended[:, :, reach_now - 1 : reach_now - 1 + columns]
        remain = driving - current
        squares = jnp.sum(remain * remain, axis=(1, 2, 3))
        records.append(by_axis(squares, GX))
    stacked = jnp.stack(records)
    return (current, jnp.sqrt(stacked / cell_count))


def solution(mesh):
    finer = Mesh(mesh.devices.reshape(mesh.shape["ens"], 4, 16, 2), ("ens", "gx_0", "gx_1", "gx_2"))
    in_specs = (P("ens", None, GX, None), P("ens", None, GX, None), P(), P(), P(), P())
    out_specs = (P("ens", None, GX, None), P("ens", None))
    return jax.shard_map(local, mesh=finer, in_specs=in_specs, out_specs=out_specs, check_vma=False)
```

profile of v0, /device:TPU:33, one launch (start us, length us, event | category | flops | bytes accessed | tf_op | source)
XLA Modules:
  0.0 493.7 jit_solution(17798823323414789324)
XLA Ops:
  0.7 3.1 copy.8
  3.8 1.9 copy-done.2
  5.7 1.2 fusion.219
  6.9 5.7 %collective-permute-start = (f32[4,4,4,2560]{3,2,1,0:T(4,128)}, f32[4,4,4,2560]{3,2,1,0:T(4,128)}, u32[]{:S(2)}, u32[]{:S(2)}) collective-permute-start(f32[4,4,4,2560]{3,2,1,0:T(4,128)} %get-tuple-element.20), channel_id=1, source_target_pairs={{0,1},{1,2},{2,3},{3,4},{4,5},{5,6},{6,7},{7,8},{8,9},{9,10},{10,1... | collective-permute-start | bytes 1966088 | tf_op jit(solution)/shard_map/ppermute | solution.py:26
  12.7 18.8 %collective-permute-start.1 = (f32[4,4,4,2560]{3,2,1,0:T(4,128)}, f32[4,4,4,2560]{3,2,1,0:T(4,128)}, u32[]{:S(2)}, u32[]{:S(2)}) collective-permute-start(f32[4,4,4,2560]{3,2,1,0:T(4,128)} %get-tuple-element.21), channel_id=1, source_target_pairs={{1,0},{2,1},{3,2},{4,3},{5,4},{6,5},{7,6},{8,7},{9,8},{10,9},{11,1... | collective-permute-start | bytes 1966088 | tf_op jit(solution)/shard_map/ppermute | solution.py:28
  31.4 0.5 compare_and_fusion.3
  32.0 0.5 compare_and_fusion.2
  32.5 0.5 fusion.168
  33.0 0.5 compare_and_fusion.1
  33.6 3.6 sub.42
  37.2 4.7 fusion.29
  42.5 0.9 copy.72
  43.3 14.7 %psum.168 = f32[4,4,30,30]{3,1,0,2:T(4,128)S(1)} all-reduce(f32[4,4,30,30]{3,1,0,2:T(4,128)} %bitcast.73), channel_id=1, replica_groups=mesh['ens'=2,'gx_0'=4,'gx_1'=16,'gx_2'=2] {'gx_0'}, use_global_device_ids=true, to_apply=%region_0.1 | all-reduce | flops 14400 | bytes 115200 | tf_op jit(solution)/shard_map/psum | solution.py:14
  58.1 0.8 convolution_bitcast_fusion.4
  58.9 47.4 %psum.169 = f32[4,4,30,30]{3,1,0,2:T(4,128)} all-reduce(f32[4,4,30,30]{3,1,0,2:T(4,128)S(1)} %psum.168), channel_id=1, replica_groups=mesh['ens'=2,'gx_0'=4,'gx_1'=16,'gx_2'=2] {'gx_1'}, use_global_device_ids=true, to_apply=%region_1.2 | all-reduce | flops 14400 | bytes 115200 | tf_op jit(solution)/shard_map/psum | solution.py:14
  106.3 0.8 copy.11
  107.1 23.6 %psum.170 = f32[4,4,30,30]{3,1,0,2:T(4,128)S(1)} all-reduce(f32[4,4,30,30]{3,1,0,2:T(4,128)} %psum.169), channel_id=1, replica_groups=mesh['ens'=2,'gx_0'=4,'gx_1'=16,'gx_2'=2] {'gx_2'}, use_global_device_ids=true, to_apply=%region_2.3 | all-reduce | flops 14400 | bytes 115200 | tf_op jit(solution)/shard_map/psum | solution.py:14
  130.7 0.5 fusion.167
  131.2 0.6 convolution_bitcast_fusion
  131.8 3.2 pad_maximum_fusion
  135.0 0.9 slice.106
  136.0 6.8 %fusion.5 = f32[4,4,26,2560]{3,2,1,0:T(8,128)S(1)} fusion(f32[4,4,26,2560]{3,2,1,0:T(8,128)S(1)} %slice.106, f32[4,4,28,2560]{3,2,1,0:T(8,128)S(1)} %pad_maximum_fusion, f32[4,4,26,30]{3,2,1,0:T(8,128)S(1)} %convolution_bitcast_fusion, f32[4,4]{1,0:T(4,128)S(1)} %copy.11, pred[26]{0:T(512)(128)(4,1)S(1)} %compare_and_fusion, s32[2560]{0:T(1024)S(1)} %iota_add_fusion, ...), kind=kOutput, calls=%fused_computation.7 | convolution fusion | flops 394726400 | bytes 17099730 | tf_op jit(solution)/shard_map/dot_general | solution.py:91
  142.8 5.7 %fusion.32 = f32[4,4,20,30]{3,2,1,0:T(8,128)S(1)} fusion(f32[4,4,20,2560]{3,1,2,0:T(4,128)S(1)} %copy-done.1, f32[4,4,26,2560]{3,2,1,0:T(8,128)S(1)} %fusion.5, s32[2560]{0:T(1024)S(1)} %iota_add_fusion, s32[30]{0:T(128)S(1)} %copy-done.7), kind=kOutput, calls=%fused_computation.55 | convolution fusion | flops 296422400 | bytes 7260160 | tf_op jit(solution)/shard_map/dot_general | solution.py:71
  148.5 2.5 slice.109
  151.7 14.8 %psum.171 = f32[4,4,30,30]{3,1,0,2:T(4,128)} all-reduce(f32[4,4,30,30]{3,1,0,2:T(4,128)S(1)} %bitcast.74), channel_id=1, replica_groups=mesh['ens'=2,'gx_0'=4,'gx_1'=16,'gx_2'=2] {'gx_0'}, use_global_device_ids=true, to_apply=%region_3.4 | all-reduce | flops 14400 | bytes 115200 | tf_op jit(solution)/shard_map/psum | solution.py:14
  166.5 42.7 %psum.172 = f32[4,4,30,30]{3,1,0,2:T(4,128)} all-reduce(f32[4,4,30,30]{3,1,0,2:T(4,128)} %psum.171), channel_id=1, replica_groups=mesh['ens'=2,'gx_0'=4,'gx_1'=16,'gx_2'=2] {'gx_1'}, use_global_device_ids=true, to_apply=%region_4.5 | all-reduce | flops 14400 | bytes 115200 | tf_op jit(solution)/shard_map/psum | solution.py:14
  209.2 21.6 %psum.173 = f32[4,4,30,30]{3,1,0,2:T(4,128)S(1)} all-reduce(f32[4,4,30,30]{3,1,0,2:T(4,128)} %psum.172), channel_id=1, replica_groups=mesh['ens'=2,'gx_0'=4,'gx_1'=16,'gx_2'=2] {'gx_2'}, use_global_device_ids=true, to_apply=%region_5.6 | all-reduce | flops 14400 | bytes 115200 | tf_op jit(solution)/shard_map/psum | solution.py:14
  230.8 1.2 convolution_bitcast_fusion.3
  232.0 10.2 %fusion.12 = f32[4,4,24,2560]{3,2,1,0:T(8,128)S(1)} fusion(f32[4,4,24,2560]{3,2,1,0:T(8,128)} %slice.109, f32[4,4,24,30]{3,2,1,0:T(8,128)S(1)} %convolution_bitcast_fusion.3, f32[4,4,26,2560]{3,2,1,0:T(8,128)} %copy-done.5, f32[4,4]{1,0:T(4,128)S(1)} %copy.11, pred[24]{0:T(512)(128)(4,1)} %compare_and_fusion.1, s32[2560]{0:T(1024)S(1)} %iota_add_fusion, ...), kind=kOutput, calls=%fused_computation.19 | convolution fusion | flops 364416000 | bytes 15785168 | tf_op jit(solution)/shard_map/dot_general | solution.py:91
  242.2 5.2 %fusion.33 = f32[4,4,20,30]{3,2,1,0:T(8,128)S(1)} fusion(f32[4,4,20,2560]{3,1,2,0:T(4,128)S(1)} %copy-done.1, f32[4,4,24,2560]{3,2,1,0:T(8,128)S(1)} %fusion.12, s32[2560]{0:T(1024)S(1)} %iota_add_fusion, s32[30]{0:T(128)S(1)} %copy-done.7), kind=kOutput, calls=%fused_computation.56 | convolution fusion | flops 296422400 | bytes 7257720 | tf_op jit(solution)/shard_map/dot_general | solution.py:71
  247.4 2.5 slice.113
  250.5 16.3 %psum.174 = f32[4,4,30,30]{3,1,0,2:T(4,128)} all-reduce(f32[4,4,30,30]{3,1,0,2:T(4,128)S(1)} %bitcast.75), channel_id=1, replica_groups=mesh['ens'=2,'gx_0'=4,'gx_1'=16,'gx_2'=2] {'gx_0'}, use_global_device_ids=true, to_apply=%region_6.7 | all-reduce | flops 14400 | bytes 115200 | tf_op jit(solution)/shard_map/psum | solution.py:14
  266.8 43.6 %psum.175 = f32[4,4,30,30]{3,1,0,2:T(4,128)} all-reduce(f32[4,4,30,30]{3,1,0,2:T(4,128)} %psum.174), channel_id=1, replica_groups=mesh['ens'=2,'gx_0'=4,'gx_1'=16,'gx_2'=2] {'gx_1'}, use_global_device_ids=true, to_apply=%region_7.8 | all-reduce | flops 14400 | bytes 115200 | tf_op jit(solution)/shard_map/psum | solution.py:14
  310.5 22.8 %psum.176 = f32[4,4,30,30]{3,1,0,2:T(4,128)S(1)} all-reduce(f32[4,4,30,30]{3,1,0,2:T(4,128)} %psum.175), channel_id=1, replica_groups=mesh['ens'=2,'gx_0'=4,'gx_1'=16,'gx_2'=2] {'gx_2'}, use_global_device_ids=true, to_apply=%region_8.9 | all-reduce | flops 14400 | bytes 115200 | tf_op jit(solution)/shard_map/psum | solution.py:14
  333.3 1.1 convolution_bitcast_fusion.2
  334.4 9.9 %fusion.13 = f32[4,4,22,2560]{3,2,1,0:T(8,128)S(1)} fusion(f32[4,4,22,2560]{3,2,1,0:T(8,128)} %slice.113, f32[4,4,22,30]{3,2,1,0:T(8,128)S(1)} %convolution_bitcast_fusion.2, f32[4,4,24,2560]{3,2,1,0:T(8,128)} %copy-done.3, f32[4,4]{1,0:T(4,128)S(1)} %copy.11, pred[22]{0:T(512)(128)(4,1)} %compare_and_fusion.2, s32[2560]{0:T(1024)S(1)} %iota_add_fusion, ...), kind=kOutput, calls=%fused_computation.20 | convolution fusion | flops 334105600 | bytes 14470606 | tf_op jit(solution)/shard_map/dot_general | solution.py:91
  344.4 5.2 %fusion.31 = f32[4,4,20,30]{3,2,1,0:T(8,128)S(1)} fusion(f32[4,4,20,2560]{3,1,2,0:T(4,128)S(1)} %copy-done.1, s32[2560]{0:T(1024)S(1)} %iota_add_fusion, s32[30]{0:T(128)S(1)} %copy-done.7, f32[4,4,22,2560]{3,2,1,0:T(8,128)S(1)} %fusion.13), kind=kOutput, calls=%fused_computation.54 | convolution fusion | flops 296422400 | bytes 6930040 | tf_op jit(solution)/shard_map/dot_general | solution.py:71
  349.6 2.4 slice.117
  352.7 14.7 %psum.177 = f32[4,4,30,30]{3,1,0,2:T(4,128)} all-reduce(f32[4,4,30,30]{3,1,0,2:T(4,128)S(1)} %bitcast.76), channel_id=1, replica_groups=mesh['ens'=2,'gx_0'=4,'gx_1'=16,'gx_2'=2] {'gx_0'}, use_global_device_ids=true, to_apply=%region_9.10 | all-reduce | flops 14400 | bytes 115200 | tf_op jit(solution)/shard_map/psum | solution.py:14
  367.4 42.9 %psum.178 = f32[4,4,30,30]{3,1,0,2:T(4,128)} all-reduce(f32[4,4,30,30]{3,1,0,2:T(4,128)} %psum.177), channel_id=1, replica_groups=mesh['ens'=2,'gx_0'=4,'gx_1'=16,'gx_2'=2] {'gx_1'}, use_global_device_ids=true, to_apply=%region_10.11 | all-reduce | flops 14400 | bytes 115200 | tf_op jit(solution)/shard_map/psum | solution.py:14
  410.2 22.0 %psum.179 = f32[4,4,30,30]{3,1,0,2:T(4,128)S(1)} all-reduce(f32[4,4,30,30]{3,1,0,2:T(4,128)} %psum.178), channel_id=1, replica_groups=mesh['ens'=2,'gx_0'=4,'gx_1'=16,'gx_2'=2] {'gx_2'}, use_global_device_ids=true, to_apply=%region_11.12 | all-reduce | flops 14400 | bytes 115200 | tf_op jit(solution)/shard_map/psum | solution.py:14
  432.2 0.5 convolution_bitcast_fusion.1
  432.7 15.7 %multiply_reduce_fusion.2 = (f32[4]{0:T(128)S(1)}, f32[4]{0:T(128)S(1)}, f32[4]{0:T(128)S(1)}, f32[4]{0:T(128)S(1)}, f32[4,4,20,2560]{3,2,1,0:T(8,128)S(1)}) fusion(f32[4,4,26,2560]{3,2,1,0:T(8,128)} %copy-done.5, f32[4,4,20,2560]{3,1,2,0:T(4,128)S(1)} %copy-done.1, f32[4,4,24,2560]{3,2,1,0:T(8,128)} %copy-done.3, f32[4,4,22,2560]{3,2,1,0:T(8,128)} %copy-done.4, ...), kind=kOutput, calls=%fused_computation.53 | convolution fusion | flops 313625600 | bytes 26263308 | tf_op jit(solution)/shard_map/dot_general | solution.py:91
  448.4 3.8 copy.19
  452.2 7.7 %all-reduce.5 = (f32[4]{0:T(128)S(1)}, f32[4]{0:T(128)S(1)}, f32[4]{0:T(128)S(1)}, f32[4]{0:T(128)S(1)}) all-reduce(f32[4]{0:T(128)S(1)} %get-tuple-element.7, f32[4]{0:T(128)S(1)} %get-tuple-element.6, f32[4]{0:T(128)S(1)} %get-tuple-element.5, f32[4]{0:T(128)S(1)} %get-tuple-element.4), channel_id=1, replica_groups=mesh['ens'=2,'gx_0'=4,'gx_1'=16,'gx_2'=2] {'gx_0'}, use_global_device_ids=true, to_apply=%region_25.26 | all-reduce | flops 16 | bytes 128 | tf_op jit(solution)/shard_map/psum | solution.py:14
  459.9 21.4 %all-reduce.4 = (f32[4]{0:T(128)S(1)}, f32[4]{0:T(128)S(1)}, f32[4]{0:T(128)S(1)}, f32[4]{0:T(128)S(1)}) all-reduce(f32[4]{0:T(128)S(1)} %get-tuple-element.12, f32[4]{0:T(128)S(1)} %get-tuple-element.13, f32[4]{0:T(128)S(1)} %get-tuple-element.14, ...), channel_id=1, replica_groups=mesh['ens'=2,'gx_0'=4,'gx_1'=16,'gx_2'=2] {'gx_1'}, use_global_device_ids=true, to_apply=%region_26.27 | all-reduce | flops 16 | bytes 128 | tf_op jit(solution)/shard_map/psum | solution.py:14
  481.3 11.6 %all-reduce.6 = (f32[1,4]{1,0:T(1,128)S(1)}, f32[1,4]{1,0:T(1,128)S(1)}, f32[1,4]{1,0:T(1,128)S(1)}, f32[1,4]{1,0:T(1,128)S(1)}) all-reduce(f32[1,4]{1,0:T(1,128)S(1)} %bitcast.77, f32[1,4]{1,0:T(1,128)S(1)} %bitcast.78, f32[1,4]{1,0:T(1,128)S(1)} %bitcast.79, ...), channel_id=1, replica_groups=mesh['ens'=2,'gx_0'=4,'gx_1'=16,'gx_2'=2] {'gx_2'}, use_global_device_ids=true, to_apply=%region_27.28 | all-reduce | flops 16 | bytes 128 | tf_op jit(solution)/shard_map/psum | solution.py:14
  492.9 0.6 fusion.164
  (30 shorter events, 2.5 us)
Async XLA Ops:
  0.6 57.4 %copy-start = (f32[8,4]{0,1:T(4,128)S(1)}, f32[8,4]{0,1:T(4,128)}, u32[]{:S(2)}) copy-start(f32[8,4]{0,1:T(4,128)} %param.11) | copy-start | bytes 388
  0.6 32.9 %copy-start.1 = (f32[4,4,20,2560]{3,1,2,0:T(4,128)S(1)}, f32[4,4,20,2560]{3,1,2,0:T(4,128)}, u32[]{:S(2)}) copy-start(f32[4,4,20,2560]{3,1,2,0:T(4,128)} %param.7) | copy-start | bytes 9830404
  3.8 1.9 copy-start.2
  6.9 124.9 %collective-permute-start = (f32[4,4,4,2560]{3,2,1,0:T(4,128)}, f32[4,4,4,2560]{3,2,1,0:T(4,128)}, u32[]{:S(2)}, u32[]{:S(2)}) collective-permute-start(f32[4,4,4,2560]{3,2,1,0:T(4,128)} %get-tuple-element.20), channel_id=1, source_target_pairs={{0,1},{1,2},{2,3},{3,4},{4,5},{5,6},{6,7},{7,8},{8,9},{9,10},{10,1... | collective-permute-start | bytes 1966088 | tf_op jit(solution)/shard_map/ppermute | solution.py:26
  12.7 119.2 %collective-permute-start.1 = (f32[4,4,4,2560]{3,2,1,0:T(4,128)}, f32[4,4,4,2560]{3,2,1,0:T(4,128)}, u32[]{:S(2)}, u32[]{:S(2)}) collective-permute-start(f32[4,4,4,2560]{3,2,1,0:T(4,128)} %get-tuple-element.21), channel_id=1, source_target_pairs={{1,0},{2,1},{3,2},{4,3},{5,4},{6,5},{7,6},{8,7},{9,8},{10,9},{11,1... | collective-permute-start | bytes 1966088 | tf_op jit(solution)/shard_map/ppermute | solution.py:28
  33.6 3.6 copy-start.7
  37.2 4.8 copy-start.6
  37.2 20.9 %copy-start.8 = (s32[4]{0:T(128)S(1)}, s32[4]{0:T(128)}, u32[]{:S(2)}) copy-start(s32[4]{0:T(128)} %param.10) | copy-start | bytes 52
  142.8 5.7 %copy-start.5 = (f32[4,4,26,2560]{3,2,1,0:T(8,128)}, f32[4,4,26,2560]{3,2,1,0:T(8,128)S(1)}, u32[]{:S(2)}) copy-start(f32[4,4,26,2560]{3,2,1,0:T(8,128)S(1)} %fusion.5) | copy-start | bytes 12779524
  242.2 5.2 %copy-start.3 = (f32[4,4,24,2560]{3,2,1,0:T(8,128)}, f32[4,4,24,2560]{3,2,1,0:T(8,128)S(1)}, u32[]{:S(2)}) copy-start(f32[4,4,24,2560]{3,2,1,0:T(8,128)S(1)} %fusion.12) | copy-start | bytes 11796484
  344.3 5.2 %copy-start.4 = (f32[4,4,22,2560]{3,2,1,0:T(8,128)}, f32[4,4,22,2560]{3,2,1,0:T(8,128)S(1)}, u32[]{:S(2)}) copy-start(f32[4,4,22,2560]{3,2,1,0:T(8,128)S(1)} %fusion.13) | copy-start | bytes 10813444
where the time goes:
time: 502 us; the launch traced here: 494 us
  blocking collectives  368 us (73%)
  matrix products  69.6 us (14%)
  starting transfers between devices  24.5 us (5%)
  local copies, waits for them, and re-layouts  20.5 us (4%)
  other arithmetic  10.1 us (2%)
    psum x15, blocking collectives, by_axis(): value = lax.psum(value, axis)  368 us
    dot_general x4, matrix products, local(): jnp.dot(partial_value.reshape(-1, partial_value.shape[-1]), table_north,...  42.6 us
    dot_general x4, matrix products, local(): jnp.dot((driving - current).reshape(-1, north_cells), table_north.T, prec...  20.8 us
    ppermute x1, starting transfers between devices, extended_2(): lax.ppermute(head, axis, [((i + 1) % count, i) for i in range(ends)])  18.8 us
    unnamed x24, local copies, waits for them, and re-layouts  10.2 us
  transfers between devices with their start and end apart: 2, of which 0 were waited for; matrix products, arithmetic and copies ran while one was open for 3% of the time, Pallas kernels for 0%

commit v1 on v0

--- a/solution.py
+++ b/solution.py
@@ -11,7 +11,7 @@
 
 def by_axis(value, axes):
     for axis in axes:
-        value = lax.psum(value, axis)
+        value = jnp.sum(lax.all_gather(value, axis), axis=0)
     return value
 
 

time: 502 us -> 526 us (1.048)
  other arithmetic: 10.1 us -> 33.8 us
  blocking collectives: 368 us -> 358 us
  local copies, waits for them, and re-layouts: 20.5 us -> 28.8 us
    psum x15 -> x0, blocking collectives: 368 us -> none  [by_axis(): value = lax.psum(value, axis)]
    all_gather x0 -> x12, blocking collectives: none -> 320 us  [by_axis(): value = jnp.sum(lax.all_gather(value, axis), axis=0)]
    unnamed x0 -> x3, blocking collectives: none -> 38 us
    reduce_sum x0 -> x24, other arithmetic: none -> 23.1 us  [by_axis(): value = jnp.sum(lax.all_gather(value, axis), axis=0)]
    unnamed x24 -> x53, local copies, waits for them, and re-layouts: 10.2 us -> 17.6 us
  transfers between devices with their start and end apart: 2 -> 2, of which waited for: 0 -> 0; matrix products, arithmetic and copies ran while one was open for 3% -> 5% of each run, Pallas kernels for 0% -> 0%
where the time goes in v1:
time: 526 us; the launch traced here: 518 us
  blocking collectives  358 us (68%)
  matrix products  69.3 us (13%)
  other arithmetic  33.8 us (6%)
  local copies, waits for them, and re-layouts  28.8 us (5%)
  starting transfers between devices  24.5 us (5%)
    all_gather x12, blocking collectives, by_axis(): value = jnp.sum(lax.all_gather(value, axis), axis=0)  320 us
    dot_general x4, matrix products, local(): jnp.dot(partial_value.reshape(-1, partial_value.shape[-1]), table_north,...  43.8 us
    unnamed x3, blocking collectives  38 us
    reduce_sum x24, other arithmetic, by_axis(): value = jnp.sum(lax.all_gather(value, axis), axis=0)  23.1 us
    dot_general x4, matrix products, local(): jnp.dot((driving - current).reshape(-1, north_cells), table_north.T, prec...  20.6 us
    ppermute x1, starting transfers between devices, extended_2(): lax.ppermute(head, axis, [((i + 1) % count, i) for i in range(ends)])  18.8 us
    unnamed x53, local copies, waits for them, and re-layouts  17.6 us
  transfers between devices with their start and end apart: 2, of which 0 were waited for; matrix products, arithmetic and copies ran while one was open for 5% of the time, Pallas kernels for 0%

profile of v1, /device:TPU:33, one launch (start us, length us, event | category | flops | bytes accessed | tf_op | source)
XLA Modules:
  0.0 517.6 jit_solution(4420508343066100040)
XLA Ops:
  0.7 3.1 copy.49
  3.8 1.9 copy-done.3
  5.7 1.2 fusion.223
  6.9 5.7 %collective-permute-start = (f32[4,4,4,2560]{3,2,1,0:T(4,128)}, f32[4,4,4,2560]{3,2,1,0:T(4,128)}, u32[]{:S(2)}, u32[]{:S(2)}) collective-permute-start(f32[4,4,4,2560]{3,2,1,0:T(4,128)} %get-tuple-element.26), channel_id=1, source_target_pairs={{0,1},{1,2},{2,3},{3,4},{4,5},{5,6},{6,7},{7,8},{8,9},{9,10},{10,1... | collective-permute-start | bytes 1966088 | tf_op jit(solution)/shard_map/ppermute | solution.py:26
  12.7 18.8 %collective-permute-start.1 = (f32[4,4,4,2560]{3,2,1,0:T(4,128)}, f32[4,4,4,2560]{3,2,1,0:T(4,128)}, u32[]{:S(2)}, u32[]{:S(2)}) collective-permute-start(f32[4,4,4,2560]{3,2,1,0:T(4,128)} %get-tuple-element.27), channel_id=1, source_target_pairs={{1,0},{2,1},{3,2},{4,3},{5,4},{6,5},{7,6},{8,7},{9,8},{10,9},{11,1... | collective-permute-start | bytes 1966088 | tf_op jit(solution)/shard_map/ppermute | solution.py:28
  32.6 3.6 sub.42
  36.2 4.7 fusion.29
  41.7 11.6 %all-gather = f32[16,4,30,30]{3,1,2,0:T(4,128)} all-gather(f32[4,4,30,30]{3,1,2,0:T(4,128)S(1)} %copy.53), channel_id=2, replica_groups=mesh['ens'=2,'gx_0'=4,'gx_1'=16,'gx_2'=2] {'gx_0'}, dimensions={0}, use_global_device_ids=true | all-gather | bytes 288000 | tf_op jit(solution)/shard_map/all_gather | solution.py:14
  53.3 1.5 reduce_sum.252
  54.8 60.8 %all-gather.1 = f32[64,4,30,30]{3,1,2,0:T(4,128)} all-gather(f32[4,4,30,30]{3,1,2,0:T(4,128)S(1)} %reduce_sum.252), channel_id=3, replica_groups=mesh['ens'=2,'gx_0'=4,'gx_1'=16,'gx_2'=2] {'gx_1'}, dimensions={0}, use_global_device_ids=true | all-gather | bytes 979200 | tf_op jit(solution)/shard_map/all_gather | solution.py:14
  115.6 3.0 reduce_sum.253
  118.6 11.1 %all-gather.2 = f32[8,4,30,30]{3,1,2,0:T(4,128)} all-gather(f32[4,4,30,30]{3,1,2,0:T(4,128)S(1)} %reduce_sum.253), channel_id=4, replica_groups=mesh['ens'=2,'gx_0'=4,'gx_1'=16,'gx_2'=2] {'gx_2'}, dimensions={0}, use_global_device_ids=true | all-gather | bytes 172800 | tf_op jit(solution)/shard_map/all_gather | solution.py:14
  129.9 1.3 dynamic-slice
  131.2 1.3 dynamic-slice.1
  133.7 1.3 dynamic-slice.2
  135.7 1.2 reduce_sum.254
  140.2 3.2 pad_maximum_fusion
  144.4 6.8 %fusion.5 = f32[4,4,26,2560]{3,2,1,0:T(8,128)S(1)} fusion(f32[4,4,26,2560]{3,2,1,0:T(8,128)S(1)} %slice.106, f32[4,4,28,2560]{3,2,1,0:T(8,128)S(1)} %pad_maximum_fusion, f32[4,4,26,30]{3,2,1,0:T(8,128)S(1)} %convolution_bitcast_fusion, f32[4,4]{1,0:T(4,128)S(1)} %copy.55, pred[26]{0:T(512)(128)(4,1)S(1)} %copy-done.11, s32[2560]{0:T(1024)S(1)} %iota_add_fusion, ...), kind=kOutput, calls=%fused_computation.7 | convolution fusion | flops 394726400 | bytes 17099730 | tf_op jit(solution)/shard_map/dot_general | solution.py:91
  151.3 5.4 %fusion.32 = f32[4,4,20,30]{3,2,1,0:T(8,128)S(1)} fusion(f32[4,4,20,2560]{3,1,2,0:T(4,128)S(1)} %copy-done.2, f32[4,4,26,2560]{3,2,1,0:T(8,128)S(1)} %fusion.5, s32[2560]{0:T(1024)S(1)} %iota_add_fusion, s32[30]{0:T(128)S(1)} %copy-done.8), kind=kOutput, calls=%fused_computation.55 | convolution fusion | flops 296422400 | bytes 7260160 | tf_op jit(solution)/shard_map/dot_general | solution.py:71
  156.7 2.5 slice.109
  159.9 12.7 %all-gather.3 = f32[16,4,30,30]{3,1,2,0:T(4,128)} all-gather(f32[4,4,30,30]{3,1,2,0:T(4,128)S(1)} %copy.57), channel_id=5, replica_groups=mesh['ens'=2,'gx_0'=4,'gx_1'=16,'gx_2'=2] {'gx_0'}, dimensions={0}, use_global_device_ids=true | all-gather | bytes 288000 | tf_op jit(solution)/shard_map/all_gather | solution.py:14
  172.7 1.5 reduce_sum.255
  174.2 52.5 %all-gather.4 = f32[64,4,30,30]{3,1,2,0:T(4,128)} all-gather(f32[4,4,30,30]{3,1,2,0:T(4,128)S(1)} %reduce_sum.255), channel_id=6, replica_groups=mesh['ens'=2,'gx_0'=4,'gx_1'=16,'gx_2'=2] {'gx_1'}, dimensions={0}, use_global_device_ids=true | all-gather | bytes 979200 | tf_op jit(solution)/shard_map/all_gather | solution.py:14
  226.7 3.0 reduce_sum.256
  229.7 13.2 %all-gather.5 = f32[8,4,30,30]{3,1,2,0:T(4,128)} all-gather(f32[4,4,30,30]{3,1,2,0:T(4,128)S(1)} %reduce_sum.256), channel_id=7, replica_groups=mesh['ens'=2,'gx_0'=4,'gx_1'=16,'gx_2'=2] {'gx_2'}, dimensions={0}, use_global_device_ids=true | all-gather | bytes 172800 | tf_op jit(solution)/shard_map/all_gather | solution.py:14
  242.9 1.2 reduce_sum.257
  244.6 10.2 %fusion.12 = f32[4,4,24,2560]{3,2,1,0:T(8,128)S(1)} fusion(f32[4,4,24,2560]{3,2,1,0:T(8,128)} %slice.109, f32[4,4,24,30]{3,2,1,0:T(8,128)S(1)} %convolution_bitcast_fusion.3, f32[4,4,26,2560]{3,2,1,0:T(8,128)} %copy-done.6, f32[4,4]{1,0:T(4,128)S(1)} %copy.55, pred[24]{0:T(512)(128)(4,1)} %compare_and_fusion.1, s32[2560]{0:T(1024)S(1)} %iota_add_fusion, ...), kind=kOutput, calls=%fused_computation.19 | convolution fusion | flops 364416000 | bytes 15785168 | tf_op jit(solution)/shard_map/dot_general | solution.py:91
  254.8 5.2 %fusion.33 = f32[4,4,20,30]{3,2,1,0:T(8,128)S(1)} fusion(f32[4,4,20,2560]{3,1,2,0:T(4,128)S(1)} %copy-done.2, f32[4,4,24,2560]{3,2,1,0:T(8,128)S(1)} %fusion.12, s32[2560]{0:T(1024)S(1)} %iota_add_fusion, s32[30]{0:T(128)S(1)} %copy-done.8), kind=kOutput, calls=%fused_computation.56 | convolution fusion | flops 296422400 | bytes 7257720 | tf_op jit(solution)/shard_map/dot_general | solution.py:71
  260.0 2.5 slice.113
  263.2 12.7 %all-gather.6 = f32[16,4,30,30]{3,1,2,0:T(4,128)} all-gather(f32[4,4,30,30]{3,1,2,0:T(4,128)S(1)} %copy.61), channel_id=8, replica_groups=mesh['ens'=2,'gx_0'=4,'gx_1'=16,'gx_2'=2] {'gx_0'}, dimensions={0}, use_global_device_ids=true | all-gather | bytes 288000 | tf_op jit(solution)/shard_map/all_gather | solution.py:14
  276.0 1.5 reduce_sum.258
  277.5 51.6 %all-gather.7 = f32[64,4,30,30]{3,1,2,0:T(4,128)} all-gather(f32[4,4,30,30]{3,1,2,0:T(4,128)S(1)} %reduce_sum.258), channel_id=9, replica_groups=mesh['ens'=2,'gx_0'=4,'gx_1'=16,'gx_2'=2] {'gx_1'}, dimensions={0}, use_global_device_ids=true | all-gather | bytes 979200 | tf_op jit(solution)/shard_map/all_gather | solution.py:14
  329.1 3.0 reduce_sum.259
  332.1 13.8 %all-gather.8 = f32[8,4,30,30]{3,1,2,0:T(4,128)} all-gather(f32[4,4,30,30]{3,1,2,0:T(4,128)S(1)} %reduce_sum.259), channel_id=10, replica_groups=mesh['ens'=2,'gx_0'=4,'gx_1'=16,'gx_2'=2] {'gx_2'}, dimensions={0}, use_global_device_ids=true | all-gather | bytes 172800 | tf_op jit(solution)/shard_map/all_gather | solution.py:14
  345.9 1.2 reduce_sum.260
  347.6 9.9 %fusion.13 = f32[4,4,22,2560]{3,2,1,0:T(8,128)S(1)} fusion(f32[4,4,22,2560]{3,2,1,0:T(8,128)} %slice.113, f32[4,4,22,30]{3,2,1,0:T(8,128)S(1)} %convolution_bitcast_fusion.2, f32[4,4,24,2560]{3,2,1,0:T(8,128)} %copy-done.4, f32[4,4]{1,0:T(4,128)S(1)} %copy.55, pred[22]{0:T(512)(128)(4,1)} %compare_and_fusion.2, s32[2560]{0:T(1024)S(1)} %iota_add_fusion, ...), kind=kOutput, calls=%fused_computation.20 | convolution fusion | flops 334105600 | bytes 14470606 | tf_op jit(solution)/shard_map/dot_general | solution.py:91
  357.5 5.2 %fusion.31 = f32[4,4,20,30]{3,2,1,0:T(8,128)S(1)} fusion(f32[4,4,20,2560]{3,1,2,0:T(4,128)S(1)} %copy-done.2, s32[2560]{0:T(1024)S(1)} %iota_add_fusion, s32[30]{0:T(128)S(1)} %copy-done.8, f32[4,4,22,2560]{3,2,1,0:T(8,128)S(1)} %fusion.13), kind=kOutput, calls=%fused_computation.54 | convolution fusion | flops 296422400 | bytes 6930040 | tf_op jit(solution)/shard_map/dot_general | solution.py:71
  362.7 2.4 slice.117
  365.8 12.8 %all-gather.9 = f32[16,4,30,30]{3,1,2,0:T(4,128)} all-gather(f32[4,4,30,30]{3,1,2,0:T(4,128)S(1)} %copy.65), channel_id=11, replica_groups=mesh['ens'=2,'gx_0'=4,'gx_1'=16,'gx_2'=2] {'gx_0'}, dimensions={0}, use_global_device_ids=true | all-gather | bytes 288000 | tf_op jit(solution)/shard_map/all_gather | solution.py:14
  378.6 1.5 reduce_sum.261
  380.1 56.4 %all-gather.10 = f32[64,4,30,30]{3,1,2,0:T(4,128)} all-gather(f32[4,4,30,30]{3,1,2,0:T(4,128)S(1)} %reduce_sum.261), channel_id=12, replica_groups=mesh['ens'=2,'gx_0'=4,'gx_1'=16,'gx_2'=2] {'gx_1'}, dimensions={0}, use_global_device_ids=true | all-gather | bytes 979200 | tf_op jit(solution)/shard_map/all_gather | solution.py:14
  436.5 3.0 reduce_sum.262
  439.5 10.8 %all-gather.11 = f32[8,4,30,30]{3,1,2,0:T(4,128)} all-gather(f32[4,4,30,30]{3,1,2,0:T(4,128)S(1)} %reduce_sum.262), channel_id=13, replica_groups=mesh['ens'=2,'gx_0'=4,'gx_1'=16,'gx_2'=2] {'gx_2'}, dimensions={0}, use_global_device_ids=true | all-gather | bytes 172800 | tf_op jit(solution)/shard_map/all_gather | solution.py:14
  452.0 16.9 %multiply_reduce_fusion.2 = (f32[4]{0:T(128)S(1)}, f32[4]{0:T(128)S(1)}, f32[4]{0:T(128)S(1)}, f32[4]{0:T(128)S(1)}, f32[4,4,20,2560]{3,2,1,0:T(8,128)}) fusion(f32[4,4,26,2560]{3,2,1,0:T(8,128)} %copy-done.6, f32[4,4,20,2560]{3,1,2,0:T(4,128)S(1)} %copy-done.2, f32[4,4,24,2560]{3,2,1,0:T(8,128)} %copy-done.4, f32[4,4,22,2560]{3,2,1,0:T(8,128)} %copy-done.5, ...), kind=kOutput, calls=%fused_computation.53 | convolution fusion | flops 313625600 | bytes 26263308 | tf_op jit(solution)/shard_map/dot_general | solution.py:91
  469.7 6.1 %all-reduce.17 = (f32[16]{0:T(128)S(1)}, f32[16]{0:T(128)S(1)}, f32[16]{0:T(128)S(1)}, f32[16]{0:T(128)S(1)}) all-reduce(f32[16]{0:T(128)S(1)} %dynamic-update-slice.9, f32[16]{0:T(128)S(1)} %dynamic-update-slice.6, f32[16]{0:T(128)S(1)} %dynamic-update-slice.3, ...), channel_id=23, replica_groups=mesh['ens'=2,'gx_0'=4,'gx_1'=16,'gx_2'=2] {'gx_0'}, use_global_device_ids=true, to_apply=%add.13 | all-reduce | flops 64 | bytes 512
  477.2 20.7 %all-reduce.16 = (f32[64]{0:T(128)S(1)}, f32[64]{0:T(128)S(1)}, f32[64]{0:T(128)S(1)}, f32[64]{0:T(128)S(1)}) all-reduce(f32[64]{0:T(128)S(1)} %dynamic-update-slice.10, f32[64]{0:T(128)S(1)} %dynamic-update-slice.7, f32[64]{0:T(128)S(1)} %dynamic-update-slice.4, ...), channel_id=24, replica_groups=mesh['ens'=2,'gx_0'=4,'gx_1'=16,'gx_2'=2] {'gx_1'}, use_global_device_ids=true, to_apply=%add.14 | all-reduce | flops 256 | bytes 2048
  499.2 11.2 %all-reduce.18 = (f32[8]{0:T(128)S(1)}, f32[8]{0:T(128)S(1)}, f32[8]{0:T(128)S(1)}, f32[8]{0:T(128)S(1)}) all-reduce(f32[8]{0:T(128)S(1)} %dynamic-update-slice.11, f32[8]{0:T(128)S(1)} %dynamic-update-slice.8, f32[8]{0:T(128)S(1)} %dynamic-update-slice.5, ...), channel_id=25, replica_groups=mesh['ens'=2,'gx_0'=4,'gx_1'=16,'gx_2'=2] {'gx_2'}, use_global_device_ids=true, to_apply=%add.15 | all-reduce | flops 32 | bytes 256
  510.8 5.9 %copy.69 = f32[4,4,20,2560]{3,1,2,0:T(4,128)} copy(f32[4,4,20,2560]{3,2,1,0:T(8,128)} %get-tuple-element.28) | data formatting | bytes 6553600
  (99 shorter events, 15.6 us)
Async XLA Ops:
  0.6 129.0 %copy-start = (f32[8,4]{0,1:T(4,128)S(1)}, f32[8,4]{0,1:T(4,128)}, u32[]{:S(2)}) copy-start(f32[8,4]{0,1:T(4,128)} %param.11) | copy-start | bytes 388
  0.6 31.9 %copy-start.2 = (f32[4,4,20,2560]{3,1,2,0:T(4,128)S(1)}, f32[4,4,20,2560]{3,1,2,0:T(4,128)}, u32[]{:S(2)}) copy-start(f32[4,4,20,2560]{3,1,2,0:T(4,128)} %param.7) | copy-start | bytes 9830404
  3.8 1.9 copy-start.3
  6.9 133.3 %collective-permute-start = (f32[4,4,4,2560]{3,2,1,0:T(4,128)}, f32[4,4,4,2560]{3,2,1,0:T(4,128)}, u32[]{:S(2)}, u32[]{:S(2)}) collective-permute-start(f32[4,4,4,2560]{3,2,1,0:T(4,128)} %get-tuple-element.26), channel_id=1, source_target_pairs={{0,1},{1,2},{2,3},{3,4},{4,5},{5,6},{6,7},{7,8},{8,9},{9,10},{10,1... | collective-permute-start | bytes 1966088 | tf_op jit(solution)/shard_map/ppermute | solution.py:26
  12.7 127.6 %collective-permute-start.1 = (f32[4,4,4,2560]{3,2,1,0:T(4,128)}, f32[4,4,4,2560]{3,2,1,0:T(4,128)}, u32[]{:S(2)}, u32[]{:S(2)}) collective-permute-start(f32[4,4,4,2560]{3,2,1,0:T(4,128)} %get-tuple-element.27), channel_id=1, source_target_pairs={{1,0},{2,1},{3,2},{4,3},{5,4},{6,5},{7,6},{8,7},{9,8},{10,9},{11,1... | collective-permute-start | bytes 1966088 | tf_op jit(solution)/shard_map/ppermute | solution.py:28
  32.6 3.6 copy-start.8
  36.2 4.7 copy-start.7
  54.8 74.9 %copy-start.10 = (s32[4]{0:T(128)S(1)}, s32[4]{0:T(128)}, u32[]{:S(2)}) copy-start(s32[4]{0:T(128)} %param.10) | copy-start | bytes 52
  143.5 1.0 copy-start.11
  151.3 5.4 %copy-start.6 = (f32[4,4,26,2560]{3,2,1,0:T(8,128)}, f32[4,4,26,2560]{3,2,1,0:T(8,128)S(1)}, u32[]{:S(2)}) copy-start(f32[4,4,26,2560]{3,2,1,0:T(8,128)S(1)} %fusion.5) | copy-start | bytes 12779524
  254.8 5.2 %copy-start.4 = (f32[4,4,24,2560]{3,2,1,0:T(8,128)}, f32[4,4,24,2560]{3,2,1,0:T(8,128)S(1)}, u32[]{:S(2)}) copy-start(f32[4,4,24,2560]{3,2,1,0:T(8,128)S(1)} %fusion.12) | copy-start | bytes 11796484
  277.5 69.6 %copy-start.9 = (s32[22]{0:T(128)S(1)}, s32[22]{0:T(128)}, u32[]{:S(2)}) copy-start(s32[22]{0:T(128)} %fusion.172) | copy-start | bytes 268
  357.5 5.3 %copy-start.5 = (f32[4,4,22,2560]{3,2,1,0:T(8,128)}, f32[4,4,22,2560]{3,2,1,0:T(8,128)S(1)}, u32[]{:S(2)}) copy-start(f32[4,4,22,2560]{3,2,1,0:T(8,128)S(1)} %fusion.13) | copy-start | bytes 10813444
  451.9 65.5 %copy-start.1 = (f32[8,4]{0,1:T(4,128)S(1)}, f32[8,4]{0,1:T(4,128)}, u32[]{:S(2)}) copy-start(f32[8,4]{0,1:T(4,128)} %param.11) | copy-start | bytes 388
